TPU v7x, 32 devices: a whole 2x2x4 slice. The times are simulated.
32 devices in a mesh: fsdp: 8 (over z, core), tp: 4 (over y, x).
Axes of the slice: x: 2, y: 2, z: 4, core: 2. Of those that a mesh axis runs over, the one named last changes fastest.
Arguments:
- tokens: bfloat16 [80, 16384], P('tp', 'fsdp'), may hold values from -6 to 6
- gate_weight: bfloat16 [16384, 28672], P('fsdp', 'tp'), may hold values from -0.046875 to 0.046875
- up_weight: bfloat16 [16384, 28672], P('fsdp', 'tp'), may hold values from -0.046875 to 0.046875
- down_weight: bfloat16 [28672, 16384], P('tp', 'fsdp'), may hold values from -0.03125 to 0.03125
Outputs:
- layer_out: bfloat16 [80, 16384], P('tp', 'fsdp')
All inputs are finite; a program needn't handle non-finite values.
Results may differ from a plain program's by a relative error of at most 0.019.
Values may be sent and summed in bfloat16 or wider, within the bound.
No kernel may reach another device: no remote copies, remote signals or barrier semaphores. Data moves between devices by JAX's collectives and lax.ppermute only.
A program may use at most 128 MiB of HBM per device.

v0:
```python
import jax
import jax.numpy as jnp
from jax import lax
from jax.sharding import PartitionSpec as P


def per_device(tokens, gate_weight, up_weight, down_weight):
    segment = lax.all_gather(tokens, "tp", axis=0, tiled=True)
    gate_part = jnp.dot(segment, gate_weight, preferred_element_type=jnp.float32)
    up_part = jnp.dot(segment, up_weight, preferred_element_type=jnp.float32)
    partials = jnp.stack([gate_part, up_part])
    summed = lax.psum_scatter(partials, "fsdp", scatter_dimension=2, tiled=True)
    hidden = (jax.nn.silu(summed[0]) * summed[1]).astype(jnp.bfloat16)
    outputs = jnp.dot(
        lax.all_gather(hidden, "fsdp", axis=1, tiled=True),
        down_weight,
        preferred_element_type=jnp.float32,
    )
    return lax.psum_scatter(outputs.astype(jnp.bfloat16), "tp", scatter_dimension=0, tiled=True)


def solution(mesh):
    placed = (P("tp", "fsdp"), P("fsdp", "tp"), P("fsdp", "tp"), P("tp", "fsdp"))
    return jax.shard_map(
        per_device, mesh=mesh, in_specs=placed, out_specs=P("tp", "fsdp"), check_vma=False
    )
```

profile of v0, /device:TPU:0, one launch (start us, length us, event | category | flops | bytes accessed | tf_op | source)
XLA Modules:
  0.0 188.8 jit_solution(4013773835530704543)
XLA Ops:
  6.5 0.0 reduce-scatter.2.cloned.1.call-start
  6.5 11.3 %all-gather = bf16[4,20,2048]{2,1,0:T(8,128)(2,1)S(1)} all-gather(bf16[1,20,2048]{2,1,0:T(8,128)(2,1)} %bitcast.22), channel_id=1, replica_groups=mesh['fsdp'=8,'tp'=4] {'tp'}, dimensions={0}, use_global_device_ids=true | all-gather | bytes 409600 | tf_op jit(solution)/shard_map/all_gather | solution.py:8
  17.9 0.1 reshape.1
  17.9 12.0 %convolution_bitcast_fusion = f32[1,80,7168]{2,1,0:T(8,128)S(1)} fusion(bf16[80,2048]{1,0:T(8,128)(2,1)S(1)} %reshape.1, bf16[2048,7168]{1,0:T(8,128)(2,1)} %param.6), kind=kOutput, calls=%fused_computation | convolution fusion | flops 2348810240 | bytes 31981568 | tf_op jit(solution)/shard_map/dot_general | solution.py:10
  29.9 12.0 %convolution_bitcast_fusion.1 = f32[1,80,7168]{2,1,0:T(8,128)S(1)} fusion(bf16[80,2048]{1,0:T(8,128)(2,1)S(1)} %reshape.1, bf16[2048,7168]{1,0:T(8,128)(2,1)} %param.5), kind=kOutput, calls=%fused_computation.1 | convolution fusion | flops 2348810240 | bytes 31981568 | tf_op jit(solution)/shard_map/dot_general | solution.py:9
  42.0 2.4 %pad_maximum_fusion = f32[2,80,7168]{2,1,0:T(8,128)} fusion(f32[1,80,7168]{2,1,0:T(8,128)S(1)} %convolution_bitcast_fusion, f32[1,80,7168]{2,1,0:T(8,128)S(1)} %convolution_bitcast_fusion.1), kind=kLoop, calls=%fused_computation.2 | loop fusion | flops 1146880 | bytes 9175040 | tf_op jit(solution)/shard_map/stack | solution.py:11
  44.3 0.0 reduce-scatter.2.cloned.1.call-update
  44.4 0.0 all-gather.3.cloned.1.call-start
  44.4 54.0 %reduce-scatter.2.cloned.1.call-done = f32[2,80,896]{2,1,0:T(8,128)} async-done(((f32[2,80,7168]{2,1,0:T(8,128)}), f32[2,80,896]{2,1,0:T(8,128)}) %reduce-scatter.2.cloned.1.call-update) | async-done | bytes 573456 | tf_op jit(solution)/shard_map/reduce_scatter | solution.py:12
  98.4 1.8 fusion.1
  100.2 0.0 all-gather.3.cloned.1.call-update
  100.2 0.0 copy-start
  100.2 0.0 all-reduce.3.cloned.1.call-start
  100.3 21.4 %all-gather.3.cloned.1.call-done = bf16[80,7168]{1,0:T(8,128)(2,1)} async-done(((bf16[80,896]{1,0:T(8,128)(2,1)}), bf16[80,7168]{1,0:T(8,128)(2,1)}) %all-gather.3.cloned.1.call-update) | async-done | bytes 1146896 | tf_op jit(solution)/shard_map/all_gather | solution.py:15
  121.7 15.6 %convolution_convert_fusion = bf16[80,2048]{1,0:T(8,128)(2,1)} fusion(bf16[80,7168]{1,0:T(8,128)(2,1)} %all-gather.3.cloned.1.call-done, bf16[7168,2048]{1,0:T(8,128)(2,1)} %param.7), kind=kOutput, calls=%fused_computation.3 | convolution fusion | flops 2348974080 | bytes 30834688 | tf_op jit(solution)/shard_map/dot_general | solution.py:14
  137.3 0.0 all-reduce.3.cloned.1.call-update
  137.3 0.0 copy-done
  137.3 0.6 dynamic-slice
  138.6 42.1 %all-reduce.3.cloned.1.call-done = bf16[80,2048]{1,0:T(8,128)(2,1)} async-done(((bf16[80,2048]{1,0:T(8,128)(2,1)}), bf16[80,2048]{1,0:T(8,128)(2,1)}) %all-reduce.3.cloned.1.call-update) | async-done | bytes 327696
  180.7 1.6 constant_dynamic-slice_fusion
Async XLA Ops:
  6.5 91.9 %reduce-scatter.2.cloned.1.call-start = ((), (), s32[]{:S(2)}) async-start(), calls=%async_computation.1 | async-start | bytes 5160960 | tf_op jit(solution)/shard_map/reduce_scatter | solution.py:12
  44.4 77.3 %all-gather.3.cloned.1.call-start = ((), (), s32[]{:S(2)}) async-start(), calls=%async_computation.2 | async-start | bytes 1290240 | tf_op jit(solution)/shard_map/all_gather | solution.py:15
  100.2 37.1 %copy-start = (u32[32]{0:T(128)S(1)}, u32[32]{0:T(128)}, u32[]{:S(2)}) copy-start(u32[32]{0:T(128)} %constant.5) | copy-start | bytes 388
  100.2 80.4 %all-reduce.3.cloned.1.call-start = ((), (), s32[]{:S(2)}) async-start(), calls=%async_computation.3 | async-start | bytes 655360
Sparse Core Ops, SparseCore 0:
  44.5 53.8 reduce-scatter.1
  100.3 21.2 all-gather.2
  137.4 43.1 all-reduce.2
where the time goes:
time: 189 us
  waiting for transfers between devices  118 us (62%)
  matrix products  39.6 us (21%)
  between operations  13.8 us (7%)
  blocking collectives  11.3 us (6%)
  other arithmetic  4.16 us (2%)
  local copies, waits for them, and re-layouts  2.23 us (1%)
    reduce_scatter x1, waiting for transfers between devices, per_device(): summed = lax.psum_scatter(partials, 'fsdp', scatter_dimension=2, tiled=True)  54 us
    unnamed x4, waiting for transfers between devices  42.2 us
    all_gather x1, waiting for transfers between devices, per_device(): lax.all_gather(hidden, 'fsdp', axis=1, tiled=True)  21.4 us
    dot_general x1, matrix products, per_device(): jnp.dot(lax.all_gather(hidden, 'fsdp', axis=1, tiled=True), down_weight,...  15.6 us
    dot_general x1, matrix products, per_device(): up_part = jnp.dot(segment, up_weight, preferred_element_type=jnp.float32)  12 us
    dot_general x1, matrix products, per_device(): jnp.dot(segment, gate_weight, preferred_element_type=jnp.float32)  12 us
    all_gather x1, blocking collectives, per_device(): segment = lax.all_gather(tokens, 'tp', axis=0, tiled=True)  11.3 us
  transfers between devices with their start and end apart: 3, of which 3 were waited for; matrix products, arithmetic and copies ran while one was open for 0% of the time, Pallas kernels for 0%

commit v1 on v0

v1 whole, which is shorter than its diff:
```python
import jax
import jax.numpy as jnp
from jax import lax
from jax.experimental import pallas as pl
from jax.experimental.pallas import tpu as pltpu
from jax.sharding import PartitionSpec as P

F32, BF16 = jnp.float32, jnp.bfloat16


def plain(tokens, gate_weight, up_weight, down_weight):
    segment = lax.all_gather(tokens, "tp", axis=0, tiled=True)
    gate_part = jnp.dot(segment, gate_weight, preferred_element_type=F32)
    up_part = jnp.dot(segment, up_weight, preferred_element_type=F32)
    partials = jnp.stack([gate_part, up_part])
    summed = lax.psum_scatter(partials, "fsdp", scatter_dimension=2, tiled=True)
    hidden = (jax.nn.silu(summed[0]) * summed[1]).astype(BF16)
    outputs = jnp.dot(
        lax.all_gather(hidden, "fsdp", axis=1, tiled=True),
        down_weight,
        preferred_element_type=F32,
    )
    return lax.psum_scatter(outputs.astype(BF16), "tp", scatter_dimension=0, tiled=True)


def tile_of(size, most):
    return next((t for t in range(most, 0, -128) if size % t == 0), size)


def gate_up(tokens, gate, up, pick, width, adds, dtypes, name):
    rows, depth = tokens.shape
    tk = tile_of(depth, 512)
    steps = depth // tk
    count = len(adds)
    given = [a for a in adds if a is not None]

    def body(tok, g, u, *rest):
        add_refs = list(rest[: len(given)])
        outs = rest[len(given) : len(given) + count]
        acc, wg, wu, sems = rest[len(given) + count :]
        blocks = pick()
        copies = []
        for b in range(count):
            at = pl.ds(pl.multiple_of(blocks[b] * width, 128), width)
            for k in range(steps):
                i = b * steps + k
                span = pl.ds(k * tk, tk)
                pair = (
                    pltpu.make_async_copy(g.at[span, at], wg.at[i], sems.at[0, i]),
                    pltpu.make_async_copy(u.at[span, at], wu.at[i], sems.at[1, i]),
                )
                for copy in pair:
                    copy.start()
                copies.append(pair)
        for b in range(count):
            for k in range(steps):
                i = b * steps + k
                t = tok[:, k * tk : (k + 1) * tk]
                for half, w in ((0, wg), (1, wu)):
                    copies[i][half].wait()
                    part = jnp.dot(t, w[i], preferred_element_type=F32)
                    acc[half] = part if k == 0 else acc[half] + part
            value = acc[...]
            if adds[b] is not None:
                value = value + add_refs.pop(0)[...].astype(F32)
            outs[b][...] = value.astype(dtypes[b])

    vmem = pl.BlockSpec(memory_space=pltpu.VMEM)
    hbm = pl.BlockSpec(memory_space=pl.ANY)
    return pl.pallas_call(
        body,
        in_specs=[vmem, hbm, hbm] + [vmem] * len(given),
        out_specs=[vmem] * count,
        scratch_shapes=[
            pltpu.VMEM((2, rows, width), F32),
            pltpu.VMEM((count * steps, tk, width), BF16),
            pltpu.VMEM((count * steps, tk, width), BF16),
            pltpu.SemaphoreType.DMA((2, count * steps)),
        ],
        out_shape=[jax.ShapeDtypeStruct((2, rows, width), d) for d in dtypes],
        cost_estimate=pl.CostEstimate(
            flops=4 * rows * depth * width * count,
            bytes_accessed=4 * depth * width * count,
            transcendentals=0,
        ),
        name=name,
    )(tokens, gate, up, *given)


def down(hiddens, weight, pick, so_far, name, dtype=F32):
    rows, width = hiddens[0].shape
    cols = weight.shape[1]
    tn = tile_of(cols, 512)
    steps = cols // tn
    count = len(hiddens)

    def body(w, *rest):
        hs = rest[:count]
        before = rest[count] if so_far is not None else None
        out, tiles, sems = rest[-3:]
        blocks = pick()
        copies = []
        for b in range(count):
            at = pl.ds(pl.multiple_of(blocks[b] * width, 128), width)
            for j in range(steps):
                i = b * steps + j
                copy = pltpu.make_async_copy(
                    w.at[at, pl.ds(j * tn, tn)], tiles.at[i], sems.at[i]
                )
                copy.start()
                copies.append(copy)
        for b in range(count):
            for j in range(steps):
                i = b * steps + j
                span = slice(j * tn, (j + 1) * tn)
                copies[i].wait()
                part = jnp.dot(hs[b][...], tiles[i], preferred_element_type=F32)
                if b > 0:
                    part = part + out[:, span]
                elif before is not None:
                    part = part + before[:, span]
                out[:, span] = part.astype(dtype)

    vmem = pl.BlockSpec(memory_space=pltpu.VMEM)
    extra = [] if so_far is None else [so_far]
    return pl.pallas_call(
        body,
        in_specs=[pl.BlockSpec(memory_space=pl.ANY)] + [vmem] * (count + len(extra)),
        out_specs=vmem,
        scratch_shapes=[
            pltpu.VMEM((count * steps, width, tn), BF16),
            pltpu.SemaphoreType.DMA((count * steps,)),
        ],
        out_shape=jax.ShapeDtypeStruct((rows, cols), dtype),
        cost_estimate=pl.CostEstimate(
            flops=2 * rows * width * cols * count,
            bytes_accessed=2 * width * cols * count,
            transcendentals=0,
        ),
        name=name,
    )(weight, *hiddens, *extra)


def split(n, tp):
    pairs = n // 2
    swap = [(j, j ^ 1) for j in range(n)]

    def own(o):
        me = lax.axis_index("fsdp")
        return 2 * ((me // 2 + o) % pairs) + me % 2

    def other(o):
        me = lax.axis_index("fsdp")
        return 2 * ((me // 2 + o) % pairs) + 1 - me % 2

    def shift(x, o):
        perm = [(j, 2 * ((j // 2 + o) % pairs) + j % 2) for j in range(n)]
        return lax.ppermute(x, "fsdp", perm)

    def trade(x):
        return lax.ppermute(x, "fsdp", swap)

    def peer(x, k):
        return lax.ppermute(x, "tp", [(j, j ^ k) for j in range(tp)])

    return pairs, own, other, shift, trade, peer


def per_device(n, tp, tokens, gate_weight, up_weight, down_weight):
    pairs, own, other, shift, trade, peer = split(n, tp)
    width = gate_weight.shape[1] // n
    mine = tokens.shape[0]
    segment = jnp.concatenate([tokens] + [peer(tokens, k) for k in range(1, tp)])

    order = sorted(range(1, pairs), key=lambda o: (-min(o, pairs - o), o)) + [0]
    calls = [[("to", order[0]), ("to", order[1])]]
    for i in range(1, pairs - 1):
        calls.append([("at", order[i - 1]), ("to", order[i + 1])])
    if pairs > 2:
        calls[-1] = [("at", order[-3]), ("at", order[-2])]
        calls.append([("to", 0), ("at", 0)])
    else:
        calls.append([("at", order[0]), ("at", 0)])
    arrived = {}
    received = []
    for i, call in enumerate(calls):
        parts = gate_up(
            segment,
            gate_weight,
            up_weight,
            lambda: [own(o) if kind == "at" else other(o) for kind, o in call],
            width,
            [arrived[o] if kind == "at" and o else None for kind, o in call],
            [F32 if kind == "at" and not o else BF16 for kind, o in call],
            f"gu{i}",
        )
        segment, *parts = lax.optimization_barrier([segment, *parts])
        for (kind, o), part in zip(call, parts):
            if kind == "to":
                arrived[o] = trade(part)
            elif o:
                received.append(shift(part, o))
            else:
                total = part
    for part in received + [arrived[0]]:
        total = total + part.astype(F32)
    hidden = (jax.nn.silu(total[0]) * total[1]).astype(BF16)

    rest = order[:-1][::-1]
    beside = trade(hidden)
    straight = {o: shift(hidden, -o) for o in rest}
    near, far = rest[:-1], rest[-1]
    outputs = down([hidden], down_weight, lambda: [own(0)], None, "down0")
    *held, outputs = lax.optimization_barrier([straight[o] for o in near] + [outputs])
    crossed = [trade(x) for x in held]
    outputs = down(
        [beside] + held,
        down_weight,
        lambda: [other(0)] + [own(o) for o in near],
        outputs,
        "down1",
    )
    distant, outputs = lax.optimization_barrier((straight[far], outputs))
    final = trade(distant)
    outputs = down(
        crossed + [distant],
        down_weight,
        lambda: [other(o) for o in near] + [own(far)],
        outputs,
        "down2",
    )
    outputs = down([final], down_weight, lambda: [other(far)], outputs, "down3", BF16)
    rows = [outputs[k * mine : (k + 1) * mine] for k in range(tp)]
    result = rows[0].astype(F32)
    for k in range(1, tp):
        result = result + peer(rows[k], k).astype(F32)
    return result.astype(BF16)


def solution(mesh):
    n, tp = mesh.shape["fsdp"], mesh.shape["tp"]

    def body(tokens, gate_weight, up_weight, down_weight):
        width = gate_weight.shape[1] // n
        fits = n % 2 == 0 and n >= 4 and tp & (tp - 1) == 0 and width % 128 == 0
        fits = fits and tokens.shape[1] % 128 == 0 and (tp * tokens.shape[0]) % 16 == 0
        if not fits:
            return plain(tokens, gate_weight, up_weight, down_weight)
        return per_device(n, tp, tokens, gate_weight, up_weight, down_weight)

    placed = (P("tp", "fsdp"), P("fsdp", "tp"), P("fsdp", "tp"), P("tp", "fsdp"))
    return jax.shard_map(
        body, mesh=mesh, in_specs=placed, out_specs=P("tp", "fsdp"), check_vma=False
    )
```

time: 189 us -> 106 us (0.56)
  waiting for transfers between devices: 118 us -> 21.1 us
  Pallas kernels: 0 us -> 52.6 us
  matrix products: 39.6 us -> 0 us
  starting transfers between devices: 0.09 us -> 20.6 us
  between operations: 13.8 us -> 0.22 us
  blocking collectives: 11.3 us -> 0 us
  local copies, waits for them, and re-layouts: 2.23 us -> 6.02 us
    reduce_scatter x1 -> x0, waiting for transfers between devices: 54 us -> none  [per_device(): summed = lax.psum_scatter(partials, 'fsdp', scatter_dimension=2, tiled=True)]
    pallas_call x0 -> x8, Pallas kernels: none -> 52.6 us  [the longest x4 30.5 us: gate_up(): pl.pallas_call(body, in_specs=[vmem, hbm, hbm] + [vmem] * len(given), out...]
    unnamed x4 -> x0, waiting for transfers between devices: 42.2 us -> none
    dot_general x3 -> x0, matrix products: 39.6 us -> none  [the longest x1 15.6 us: per_device(): jnp.dot(lax.all_gather(hidden, 'fsdp', axis=1, tiled=True), down_weight,...]
    all_gather x1 -> x0, waiting for transfers between devices: 21.4 us -> none  [per_device(): lax.all_gather(hidden, 'fsdp', axis=1, tiled=True)]
    ppermute x0 -> x20, waiting for transfers between devices: none -> 21.1 us  [the longest x6 11.3 us: peer(): return lax.ppermute(x, 'tp', [(j, j ^ k) for j in range(tp)])]
    ppermute x0 -> x20, starting transfers between devices: none -> 20.6 us  [the longest x6 11.3 us: shift(): return lax.ppermute(x, 'fsdp', perm)]
    all_gather x1 -> x0, blocking collectives: 11.3 us -> none  [per_device(): segment = lax.all_gather(tokens, 'tp', axis=0, tiled=True)]
  transfers between devices with their start and end apart: 3 -> 20, of which waited for: 3 -> 10; matrix products, arithmetic and copies ran while one was open for 0% -> 0% of each run, Pallas kernels for 0% -> 39%
where the time goes in v1:
time: 106 us; the launch traced here: 105 us
  Pallas kernels  52.6 us (50%)
  waiting for transfers between devices  21.1 us (20%)
  starting transfers between devices  20.6 us (19%)
  local copies, waits for them, and re-layouts  6.02 us (6%)
  other arithmetic  4.6 us (4%)
    pallas_call x4, Pallas kernels, gate_up(): pl.pallas_call(body, in_specs=[vmem, hbm, hbm] + [vmem] * len(given), out...  30.5 us
    pallas_call x4, Pallas kernels, down(): pl.pallas_call(body, in_specs=[pl.BlockSpec(memory_space=pl.ANY)] + [vmem...  22.1 us
    ppermute x6, waiting for transfers between devices, peer(): return lax.ppermute(x, 'tp', [(j, j ^ k) for j in range(tp)])  11.3 us
    ppermute x6, starting transfers between devices, shift(): return lax.ppermute(x, 'fsdp', perm)  11.3 us
    ppermute x6, waiting for transfers between devices, shift(): return lax.ppermute(x, 'fsdp', perm)  8.52 us
    ppermute x6, starting transfers between devices, peer(): return lax.ppermute(x, 'tp', [(j, j ^ k) for j in range(tp)])  8.04 us
    unnamed x22, local copies, waits for them, and re-layouts  4.96 us
  transfers between devices with their start and end apart: 20, of which 10 were waited for; matrix products, arithmetic and copies ran while one was open for 0% of the time, Pallas kernels for 39%

profile of v1, /device:TPU:0, one launch (start us, length us, event | category | flops | bytes accessed | tf_op | source)
XLA Modules:
  0.0 105.2 jit_solution(10368283991608469655)
XLA Ops:
  0.0 3.0 %collective-permute-start.1 = (bf16[20,2048]{1,0:T(8,128)(2,1)}, bf16[20,2048]{1,0:T(8,128)(2,1)S(1)}, u32[]{:S(2)}, u32[]{:S(2)}) collective-permute-start(bf16[20,2048]{1,0:T(8,128)(2,1)} %param.4), channel_id=1, source_target_pairs={{0,2},{1,3},{2,0},{3,1},{4,6},{5,7},{6,4},{7,5},{8,10},{9,11},{10,... | collective-permute-start | bytes 245768 | tf_op jit(solution)/shard_map/ppermute | solution.py:164
  3.0 1.5 %collective-permute-start = (bf16[20,2048]{1,0:T(8,128)(2,1)}, bf16[20,2048]{1,0:T(8,128)(2,1)S(1)}, u32[]{:S(2)}, u32[]{:S(2)}) collective-permute-start(bf16[20,2048]{1,0:T(8,128)(2,1)} %param.4), channel_id=1, source_target_pairs={{0,1},{1,0},{2,3},{3,2},{4,5},{5,4},{6,7},{7,6},{8,9},{9,8},{10,11... | collective-permute-start | bytes 245768 | tf_op jit(solution)/shard_map/ppermute | solution.py:164
  4.5 0.0 collective-permute-start.2
  4.5 1.5 %collective-permute-done.1 = bf16[20,2048]{1,0:T(8,128)(2,1)S(1)} collective-permute-done((bf16[20,2048]{1,0:T(8,128)(2,1)}, bf16[20,2048]{1,0:T(8,128)(2,1)S(1)}, u32[]{:S(2)}, u32[]{:S(2)}) %collective-permute-start.1) | collective-permute-done | bytes 81952 | tf_op jit(solution)/shard_map/ppermute | solution.py:164
  6.0 2.6 %collective-permute-done = bf16[20,2048]{1,0:T(8,128)(2,1)S(1)} collective-permute-done((bf16[20,2048]{1,0:T(8,128)(2,1)}, bf16[20,2048]{1,0:T(8,128)(2,1)S(1)}, u32[]{:S(2)}, u32[]{:S(2)}) %collective-permute-start) | collective-permute-done | bytes 81952 | tf_op jit(solution)/shard_map/ppermute | solution.py:164
  8.6 1.6 %collective-permute-done.2 = bf16[20,2048]{1,0:T(8,128)(2,1)S(1)} collective-permute-done((bf16[20,2048]{1,0:T(8,128)(2,1)}, bf16[20,2048]{1,0:T(8,128)(2,1)S(1)}, u32[]{:S(2)}, u32[]{:S(2)}) %collective-permute-start.2) | collective-permute-done | bytes 81952 | tf_op jit(solution)/shard_map/ppermute | solution.py:164
  10.2 1.7 %pad_maximum_fusion.tok = bf16[80,2048]{1,0:T(8,128)(2,1)} fusion(bf16[20,2048]{1,0:T(8,128)(2,1)S(1)} %collective-permute-done.2, bf16[20,2048]{1,0:T(8,128)(2,1)S(1)} %collective-permute-done.1, bf16[20,2048]{1,0:T(8,128)(2,1)S(1)} %collective-permute-done, bf16[20,2048]{1,0:T(8,128)(2,1)} %param.4), kind=kLoop, calls=%fused_computation.1 | loop fusion | flops 1310720 | bytes 655360 | tf_op jit(solution)/shard_map/concatenate | solution.py:173
  11.9 7.5 %gu0.1 = (bf16[2,80,896]{2,1,0:T(8,128)(2,1)}, bf16[2,80,896]{2,1,0:T(8,128)(2,1)}) custom-call(bf16[80,2048]{1,0:T(8,128)(2,1)} %pad_maximum_fusion.tok, bf16[2048,7168]{1,0:T(8,128)(2,1)} %g.7, bf16[2048,7168]{1,0:T(8,128)(2,1)} %u.7), custom_call_target="tpu_custom_call" | custom-call | flops 1174405120 | bytes 14680064 | tf_op jit(solution)/shard_map/gu0/pallas_call | solution.py:70
  19.4 0.1 collective-permute-start.3
  19.5 0.5 collective-permute-start.4
  20.0 1.3 %collective-permute-done.3.rest_0_ = bf16[2,80,896]{2,1,0:T(8,128)(2,1)S(1)} collective-permute-done((bf16[2,80,896]{2,1,0:T(8,128)(2,1)}, bf16[2,80,896]{2,1,0:T(8,128)(2,1)S(1)}, u32[]{:S(2)}, u32[]{:S(2)}) %collective-permute-start.3) | collective-permute-done | bytes 286752 | tf_op jit(solution)/shard_map/ppermute | solution.py:161
  21.3 0.8 copy-done.3
  22.0 7.7 %gu1.1 = (bf16[2,80,896]{2,1,0:T(8,128)(2,1)}, bf16[2,80,896]{2,1,0:T(8,128)(2,1)}) custom-call(bf16[80,2048]{1,0:T(8,128)(2,1)} %pad_maximum_fusion.tok, bf16[2048,7168]{1,0:T(8,128)(2,1)} %g.7, bf16[2048,7168]{1,0:T(8,128)(2,1)} %u.7, bf16[2,80,896]{2,1,0:T(8,128)(2,1)} %copy-done.3), custom_call_target="tpu_custom_call" | custom-call | flops 1174405120 | bytes 14680064 | tf_op jit(solution)/shard_map/gu1/pallas_call | solution.py:70
  29.7 0.1 collective-permute-start.5
  29.8 2.7 %collective-permute-start.6 = (bf16[2,80,896]{2,1,0:T(8,128)(2,1)}, bf16[2,80,896]{2,1,0:T(8,128)(2,1)S(1)}, u32[]{:S(2)}, u32[]{:S(2)}) collective-permute-start(bf16[2,80,896]{2,1,0:T(8,128)(2,1)} %get-tuple-element.44), channel_id=1, source_target_pairs={{0,16},{4,20},{8,24},{12,28},{16,0},{20,4},{24,8},{28,12},{1,17},{... | collective-permute-start | bytes 860168 | tf_op jit(solution)/shard_map/ppermute | solution.py:158
  32.6 0.0 collective-permute-done.4.rest_0_
  32.6 0.0 collective-permute-done.5.rest_1_
  32.6 0.7 copy-done.1
  33.3 0.7 copy-done.2
  34.0 7.8 %gu2.1 = (bf16[2,80,896]{2,1,0:T(8,128)(2,1)}, bf16[2,80,896]{2,1,0:T(8,128)(2,1)}) custom-call(bf16[80,2048]{1,0:T(8,128)(2,1)} %pad_maximum_fusion.tok, bf16[2048,7168]{1,0:T(8,128)(2,1)} %g.7, bf16[2048,7168]{1,0:T(8,128)(2,1)} %u.7, bf16[2,80,896]{2,1,0:T(8,128)(2,1)} %copy-done.1, bf16[2,80,896]{2,1,0:T(8,128)(2,1)} %copy-done.2), custom_call_target="tpu_custom_call" | custom-call | flops 1174405120 | bytes 14680064 | tf_op jit(solution)/shard_map/gu2/pallas_call | solution.py:70
  41.7 1.7 %collective-permute-start.7 = (bf16[2,80,896]{2,1,0:T(8,128)(2,1)}, bf16[2,80,896]{2,1,0:T(8,128)(2,1)S(1)}, u32[]{:S(2)}, u32[]{:S(2)}) collective-permute-start(bf16[2,80,896]{2,1,0:T(8,128)(2,1)} %get-tuple-element.45), channel_id=1, source_target_pairs={{0,8},{4,12},{8,16},{12,20},{16,24},{20,28},{24,0},{28,4},{1,9},{5... | collective-permute-start | bytes 860168 | tf_op jit(solution)/shard_map/ppermute | solution.py:158
  43.5 2.2 %collective-permute-start.8 = (bf16[2,80,896]{2,1,0:T(8,128)(2,1)}, bf16[2,80,896]{2,1,0:T(8,128)(2,1)S(1)}, u32[]{:S(2)}, u32[]{:S(2)}) collective-permute-start(bf16[2,80,896]{2,1,0:T(8,128)(2,1)} %get-tuple-element.46), channel_id=1, source_target_pairs={{0,24},{4,28},{8,0},{12,4},{16,8},{20,12},{24,16},{28,20},{1,25},{... | collective-permute-start | bytes 860168 | tf_op jit(solution)/shard_map/ppermute | solution.py:158
  45.6 7.6 %gu3.1 = (bf16[2,80,896]{2,1,0:T(8,128)(2,1)}, f32[2,80,896]{2,1,0:T(8,128)}) custom-call(bf16[80,2048]{1,0:T(8,128)(2,1)} %pad_maximum_fusion.tok, bf16[2048,7168]{1,0:T(8,128)(2,1)} %g.7, bf16[2048,7168]{1,0:T(8,128)(2,1)} %u.7), custom_call_target="tpu_custom_call" | custom-call | flops 1174405120 | bytes 14680064 | tf_op jit(solution)/shard_map/gu3/pallas_call | solution.py:70
  53.2 0.1 collective-permute-start.9
  53.3 0.0 collective-permute-done.6
  53.3 0.2 collective-permute-done.7
  53.5 5.1 %collective-permute-done.8 = bf16[2,80,896]{2,1,0:T(8,128)(2,1)S(1)} collective-permute-done((bf16[2,80,896]{2,1,0:T(8,128)(2,1)}, bf16[2,80,896]{2,1,0:T(8,128)(2,1)S(1)}, u32[]{:S(2)}, u32[]{:S(2)}) %collective-permute-start.8) | collective-permute-done | bytes 286752 | tf_op jit(solution)/shard_map/ppermute | solution.py:158
  58.6 0.0 collective-permute-done.9
  58.6 1.2 %convert_add_fusion = f32[2,80,896]{2,1,0:T(8,128)S(1)} fusion(bf16[2,80,896]{2,1,0:T(8,128)(2,1)S(1)} %collective-permute-done.9, bf16[2,80,896]{2,1,0:T(8,128)(2,1)S(1)} %collective-permute-done.8, bf16[2,80,896]{2,1,0:T(8,128)(2,1)S(1)} %collective-permute-done.7, f32[2,80,896]{2,1,0:T(8,128)} %get-tuple-element.43, ...), kind=kLoop, calls=%fused_computation | loop fusion | flops 1146880 | bytes 2293760 | tf_op jit(solution)/shard_map/add | solution.py:206
  59.8 0.1 fusion.1.rest_0_
  59.9 3.5 %collective-permute-start.13 = (bf16[80,896]{1,0:T(8,128)(2,1)S(1)}, bf16[80,896]{1,0:T(8,128)(2,1)S(1)}, u32[]{:S(2)}, u32[]{:S(2)}) collective-permute-start(bf16[80,896]{1,0:T(8,128)(2,1)S(1)} %fusion.1.rest_0_), channel_id=1, source_target_pairs={{0,24},{4,28},{8,0},{12,4},{16,8},{20,12},{24,16},{28,20},{1,25},{... | collective-permute-start | bytes 430088 | tf_op jit(solution)/shard_map/ppermute | solution.py:158
  63.4 0.0 collective-permute-start.12
  63.4 0.0 collective-permute-start.11
  63.4 1.2 %collective-permute-start.10 = (bf16[80,896]{1,0:T(8,128)(2,1)S(1)}, bf16[80,896]{1,0:T(8,128)(2,1)S(1)}, u32[]{:S(2)}, u32[]{:S(2)}) collective-permute-start(bf16[80,896]{1,0:T(8,128)(2,1)S(1)} %fusion.1.rest_0_), channel_id=1, source_target_pairs={{0,16},{4,20},{8,24},{12,28},{16,0},{20,4},{24,8},{28,12},{1,17},{... | collective-permute-start | bytes 430088 | tf_op jit(solution)/shard_map/ppermute | solution.py:158
  64.6 4.1 %down0.1.rest_3_ = f32[80,2048]{1,0:T(8,128)} custom-call(bf16[7168,2048]{1,0:T(8,128)(2,1)} %w.7, bf16[80,896]{1,0:T(8,128)(2,1)} %copy-done), custom_call_target="tpu_custom_call" | custom-call | flops 293601280 | bytes 3670016 | tf_op jit(solution)/shard_map/down0/pallas_call | solution.py:126
  68.7 0.0 collective-permute-done.13.rest_2_
  68.8 0.0 copy-start.4
  68.8 3.2 %collective-permute-done.12.rest_1_ = bf16[80,896]{1,0:T(8,128)(2,1)S(1)} collective-permute-done((bf16[80,896]{1,0:T(8,128)(2,1)S(1)}, bf16[80,896]{1,0:T(8,128)(2,1)S(1)}, u32[]{:S(2)}, u32[]{:S(2)}) %collective-permute-start.12) | collective-permute-done | bytes 143392 | tf_op jit(solution)/shard_map/ppermute | solution.py:158
  72.0 0.0 collective-permute-start.15
  72.0 0.5 collective-permute-start.16
  72.5 0.0 collective-permute-done.11.rest_0_
  72.5 0.1 copy-done.6
  72.6 0.7 copy-done.9
  73.3 6.8 %down1.1.rest_3_ = f32[80,2048]{1,0:T(8,128)} custom-call(bf16[7168,2048]{1,0:T(8,128)(2,1)} %w.7, bf16[80,896]{1,0:T(8,128)(2,1)} %copy-done.9, bf16[80,896]{1,0:T(8,128)(2,1)} %copy-done.6, bf16[80,896]{1,0:T(8,128)(2,1)} %copy-done.4, f32[80,2048]{1,0:T(8,128)} %down0.1.rest_3_), custom_call_target="tpu_custom_call" | custom-call | flops 880803840 | bytes 11010048 | tf_op jit(solution)/shard_map/down1/pallas_call | solution.py:126
  80.1 0.0 collective-permute-done.10.rest_2_
  80.1 0.1 collective-permute-start.14
  80.2 0.0 collective-permute-done.15.rest_0_
  80.2 0.0 copy-start.7
  80.2 0.0 collective-permute-done.16.rest_1_
  80.2 0.5 copy-done.5
  80.8 0.1 copy-done.7
  80.9 0.7 copy-done.8
  81.6 6.8 %down2.1.rest_1_ = f32[80,2048]{1,0:T(8,128)} custom-call(bf16[7168,2048]{1,0:T(8,128)(2,1)} %w.7, bf16[80,896]{1,0:T(8,128)(2,1)} %copy-done.7, bf16[80,896]{1,0:T(8,128)(2,1)} %copy-done.8, bf16[80,896]{1,0:T(8,128)(2,1)} %copy-done.5, f32[80,2048]{1,0:T(8,128)} %down1.1.rest_3_), custom_call_target="tpu_custom_call" | custom-call | flops 880803840 | bytes 11010048 | tf_op jit(solution)/shard_map/down2/pallas_call | solution.py:126
  88.4 0.0 collective-permute-done.14.rest_0_
  88.4 0.7 copy-done.10
  89.1 4.3 %down3.1 = bf16[80,2048]{1,0:T(8,128)(2,1)} custom-call(bf16[7168,2048]{1,0:T(8,128)(2,1)} %w.7, bf16[80,896]{1,0:T(8,128)(2,1)} %copy-done.10, f32[80,2048]{1,0:T(8,128)} %down2.1.rest_1_), custom_call_target="tpu_custom_call" | custom-call | flops 293601280 | bytes 3670016 | tf_op jit(solution)/shard_map/down3/pallas_call | solution.py:126
  93.4 1.1 %fusion.2 = (bf16[20,2048]{1,0:T(8,128)(2,1)S(1)}, bf16[20,2048]{1,0:T(8,128)(2,1)S(1)}, bf16[20,2048]{1,0:T(8,128)(2,1)S(1)}) fusion(bf16[80,2048]{1,0:T(8,128)(2,1)} %down3.1), kind=kLoop, calls=%fused_computation.7 | loop fusion | bytes 491520 | tf_op jit(solution)/shard_map/slice | solution.py:233
  94.4 1.0 collective-permute-start.17
  95.4 1.4 %collective-permute-start.19 = (bf16[20,2048]{1,0:T(8,128)(2,1)S(1)}, bf16[20,2048]{1,0:T(8,128)(2,1)S(1)}, u32[]{:S(2)}, u32[]{:S(2)}) collective-permute-start(bf16[20,2048]{1,0:T(8,128)(2,1)S(1)} %get-tuple-element.54), channel_id=1, source_target_pairs={{0,3},{1,2},{2,1},{3,0},{4,7},{5,6},{6,5},{7,4},{8,11},{9,10},{10,... | collective-permute-start | bytes 245768 | tf_op jit(solution)/shard_map/ppermute | solution.py:164
  96.9 1.1 %collective-permute-start.18 = (bf16[20,2048]{1,0:T(8,128)(2,1)S(1)}, bf16[20,2048]{1,0:T(8,128)(2,1)S(1)}, u32[]{:S(2)}, u32[]{:S(2)}) collective-permute-start(bf16[20,2048]{1,0:T(8,128)(2,1)S(1)} %get-tuple-element.55), channel_id=1, source_target_pairs={{0,2},{1,3},{2,0},{3,1},{4,6},{5,7},{6,4},{7,5},{8,10},{9,11},{10,... | collective-permute-start | bytes 245768 | tf_op jit(solution)/shard_map/ppermute | solution.py:164
  98.0 2.2 %collective-permute-done.17 = bf16[20,2048]{1,0:T(8,128)(2,1)S(1)} collective-permute-done((bf16[20,2048]{1,0:T(8,128)(2,1)S(1)}, bf16[20,2048]{1,0:T(8,128)(2,1)S(1)}, u32[]{:S(2)}, u32[]{:S(2)}) %collective-permute-start.17) | collective-permute-done | bytes 81952 | tf_op jit(solution)/shard_map/ppermute | solution.py:164
  100.2 2.1 %collective-permute-done.19 = bf16[20,2048]{1,0:T(8,128)(2,1)S(1)} collective-permute-done((bf16[20,2048]{1,0:T(8,128)(2,1)S(1)}, bf16[20,2048]{1,0:T(8,128)(2,1)S(1)}, u32[]{:S(2)}, u32[]{:S(2)}) %collective-permute-start.19) | collective-permute-done | bytes 81952 | tf_op jit(solution)/shard_map/ppermute | solution.py:164
  102.2 1.4 %collective-permute-done.18 = bf16[20,2048]{1,0:T(8,128)(2,1)S(1)} collective-permute-done((bf16[20,2048]{1,0:T(8,128)(2,1)S(1)}, bf16[20,2048]{1,0:T(8,128)(2,1)S(1)}, u32[]{:S(2)}, u32[]{:S(2)}) %collective-permute-start.18) | collective-permute-done | bytes 81952 | tf_op jit(solution)/shard_map/ppermute | solution.py:164
  103.6 1.6 %add_convert_fusion = bf16[20,2048]{1,0:T(8,128)(2,1)} fusion(bf16[20,2048]{1,0:T(8,128)(2,1)S(1)} %collective-permute-done.19, bf16[20,2048]{1,0:T(8,128)(2,1)S(1)} %collective-permute-done.18, bf16[20,2048]{1,0:T(8,128)(2,1)S(1)} %collective-permute-done.17, bf16[80,2048]{1,0:T(8,128)(2,1)} %down3.1), kind=kLoop, calls=%fused_computation.6 | loop fusion | flops 327680 | bytes 409600 | tf_op jit(solution)/shard_map/convert_element_type | solution.py:237
  (11 shorter events, 0.0 us)
Async XLA Ops:
  0.0 6.0 %collective-permute-start.1 = (bf16[20,2048]{1,0:T(8,128)(2,1)}, bf16[20,2048]{1,0:T(8,128)(2,1)S(1)}, u32[]{:S(2)}, u32[]{:S(2)}) collective-permute-start(bf16[20,2048]{1,0:T(8,128)(2,1)} %param.4), channel_id=1, source_target_pairs={{0,2},{1,3},{2,0},{3,1},{4,6},{5,7},{6,4},{7,5},{8,10},{9,11},{10,... | collective-permute-start | bytes 245768 | tf_op jit(solution)/shard_map/ppermute | solution.py:164
  3.0 5.6 %collective-permute-start = (bf16[20,2048]{1,0:T(8,128)(2,1)}, bf16[20,2048]{1,0:T(8,128)(2,1)S(1)}, u32[]{:S(2)}, u32[]{:S(2)}) collective-permute-start(bf16[20,2048]{1,0:T(8,128)(2,1)} %param.4), channel_id=1, source_target_pairs={{0,1},{1,0},{2,3},{3,2},{4,5},{5,4},{6,7},{7,6},{8,9},{9,8},{10,11... | collective-permute-start | bytes 245768 | tf_op jit(solution)/shard_map/ppermute | solution.py:164
  4.5 5.7 %collective-permute-start.2 = (bf16[20,2048]{1,0:T(8,128)(2,1)}, bf16[20,2048]{1,0:T(8,128)(2,1)S(1)}, u32[]{:S(2)}, u32[]{:S(2)}) collective-permute-start(bf16[20,2048]{1,0:T(8,128)(2,1)} %param.4), channel_id=1, source_target_pairs={{0,3},{1,2},{2,1},{3,0},{4,7},{5,6},{6,5},{7,4},{8,11},{9,10},{10,... | collective-permute-start | bytes 245768 | tf_op jit(solution)/shard_map/ppermute | solution.py:164
  19.4 1.8 %collective-permute-start.3 = (bf16[2,80,896]{2,1,0:T(8,128)(2,1)}, bf16[2,80,896]{2,1,0:T(8,128)(2,1)S(1)}, u32[]{:S(2)}, u32[]{:S(2)}) collective-permute-start(bf16[2,80,896]{2,1,0:T(8,128)(2,1)} %get-tuple-element.32), channel_id=1, source_target_pairs={{0,4},{4,0},{8,12},{12,8},{16,20},{20,16},{24,28},{28,24},{1,5},{5... | collective-permute-start | bytes 860168 | tf_op jit(solution)/shard_map/ppermute | solution.py:161
  19.5 13.1 %collective-permute-start.4 = (bf16[2,80,896]{2,1,0:T(8,128)(2,1)}, bf16[2,80,896]{2,1,0:T(8,128)(2,1)S(1)}, u32[]{:S(2)}, u32[]{:S(2)}) collective-permute-start(bf16[2,80,896]{2,1,0:T(8,128)(2,1)} %get-tuple-element.36), channel_id=1, source_target_pairs={{0,4},{4,0},{8,12},{12,8},{16,20},{20,16},{24,28},{28,24},{1,5},{5... | collective-permute-start | bytes 860168 | tf_op jit(solution)/shard_map/ppermute | solution.py:161
  21.2 0.8 copy-start.3
  29.7 2.8 %collective-permute-start.5 = (bf16[2,80,896]{2,1,0:T(8,128)(2,1)}, bf16[2,80,896]{2,1,0:T(8,128)(2,1)S(1)}, u32[]{:S(2)}, u32[]{:S(2)}) collective-permute-start(bf16[2,80,896]{2,1,0:T(8,128)(2,1)} %get-tuple-element.37), channel_id=1, source_target_pairs={{0,4},{4,0},{8,12},{12,8},{16,20},{20,16},{24,28},{28,24},{1,5},{5... | collective-permute-start | bytes 860168 | tf_op jit(solution)/shard_map/ppermute | solution.py:161
  29.8 23.5 %collective-permute-start.6 = (bf16[2,80,896]{2,1,0:T(8,128)(2,1)}, bf16[2,80,896]{2,1,0:T(8,128)(2,1)S(1)}, u32[]{:S(2)}, u32[]{:S(2)}) collective-permute-start(bf16[2,80,896]{2,1,0:T(8,128)(2,1)} %get-tuple-element.44), channel_id=1, source_target_pairs={{0,16},{4,20},{8,24},{12,28},{16,0},{20,4},{24,8},{28,12},{1,17},{... | collective-permute-start | bytes 860168 | tf_op jit(solution)/shard_map/ppermute | solution.py:158
  32.6 0.7 copy-start.1
  33.3 0.7 copy-start.2
  41.7 11.8 %collective-permute-start.7 = (bf16[2,80,896]{2,1,0:T(8,128)(2,1)}, bf16[2,80,896]{2,1,0:T(8,128)(2,1)S(1)}, u32[]{:S(2)}, u32[]{:S(2)}) collective-permute-start(bf16[2,80,896]{2,1,0:T(8,128)(2,1)} %get-tuple-element.45), channel_id=1, source_target_pairs={{0,8},{4,12},{8,16},{12,20},{16,24},{20,28},{24,0},{28,4},{1,9},{5... | collective-permute-start | bytes 860168 | tf_op jit(solution)/shard_map/ppermute | solution.py:158
  43.5 15.2 %collective-permute-start.8 = (bf16[2,80,896]{2,1,0:T(8,128)(2,1)}, bf16[2,80,896]{2,1,0:T(8,128)(2,1)S(1)}, u32[]{:S(2)}, u32[]{:S(2)}) collective-permute-start(bf16[2,80,896]{2,1,0:T(8,128)(2,1)} %get-tuple-element.46), channel_id=1, source_target_pairs={{0,24},{4,28},{8,0},{12,4},{16,8},{20,12},{24,16},{28,20},{1,25},{... | collective-permute-start | bytes 860168 | tf_op jit(solution)/shard_map/ppermute | solution.py:158
  53.2 5.4 %collective-permute-start.9 = (bf16[2,80,896]{2,1,0:T(8,128)(2,1)}, bf16[2,80,896]{2,1,0:T(8,128)(2,1)S(1)}, u32[]{:S(2)}, u32[]{:S(2)}) collective-permute-start(bf16[2,80,896]{2,1,0:T(8,128)(2,1)} %get-tuple-element.47), channel_id=1, source_target_pairs={{0,4},{4,0},{8,12},{12,8},{16,20},{20,16},{24,28},{28,24},{1,5},{5... | collective-permute-start | bytes 860168 | tf_op jit(solution)/shard_map/ppermute | solution.py:161
  59.9 4.7 %copy-start = (bf16[80,896]{1,0:T(8,128)(2,1)}, bf16[80,896]{1,0:T(8,128)(2,1)S(1)}, u32[]{:S(2)}) copy-start(bf16[80,896]{1,0:T(8,128)(2,1)S(1)} %fusion.1.rest_0_) | copy-start | bytes 430084
  59.9 8.8 %collective-permute-start.13 = (bf16[80,896]{1,0:T(8,128)(2,1)S(1)}, bf16[80,896]{1,0:T(8,128)(2,1)S(1)}, u32[]{:S(2)}, u32[]{:S(2)}) collective-permute-start(bf16[80,896]{1,0:T(8,128)(2,1)S(1)} %fusion.1.rest_0_), channel_id=1, source_target_pairs={{0,24},{4,28},{8,0},{12,4},{16,8},{20,12},{24,16},{28,20},{1,25},{... | collective-permute-start | bytes 430088 | tf_op jit(solution)/shard_map/ppermute | solution.py:158
  63.4 8.5 %collective-permute-start.12 = (bf16[80,896]{1,0:T(8,128)(2,1)S(1)}, bf16[80,896]{1,0:T(8,128)(2,1)S(1)}, u32[]{:S(2)}, u32[]{:S(2)}) collective-permute-start(bf16[80,896]{1,0:T(8,128)(2,1)S(1)} %fusion.1.rest_0_), channel_id=1, source_target_pairs={{0,8},{4,12},{8,16},{12,20},{16,24},{20,28},{24,0},{28,4},{1,9},{5... | collective-permute-start | bytes 430088 | tf_op jit(solution)/shard_map/ppermute | solution.py:158
  63.4 9.0 %collective-permute-start.11 = (bf16[80,896]{1,0:T(8,128)(2,1)S(1)}, bf16[80,896]{1,0:T(8,128)(2,1)S(1)}, u32[]{:S(2)}, u32[]{:S(2)}) collective-permute-start(bf16[80,896]{1,0:T(8,128)(2,1)S(1)} %fusion.1.rest_0_), channel_id=1, source_target_pairs={{0,4},{4,0},{8,12},{12,8},{16,20},{20,16},{24,28},{28,24},{1,5},{5... | collective-permute-start | bytes 430088 | tf_op jit(solution)/shard_map/ppermute | solution.py:161
  63.4 16.7 %collective-permute-start.10 = (bf16[80,896]{1,0:T(8,128)(2,1)S(1)}, bf16[80,896]{1,0:T(8,128)(2,1)S(1)}, u32[]{:S(2)}, u32[]{:S(2)}) collective-permute-start(bf16[80,896]{1,0:T(8,128)(2,1)S(1)} %fusion.1.rest_0_), channel_id=1, source_target_pairs={{0,16},{4,20},{8,24},{12,28},{16,0},{20,4},{24,8},{28,12},{1,17},{... | collective-permute-start | bytes 430088 | tf_op jit(solution)/shard_map/ppermute | solution.py:158
  68.8 3.7 %copy-start.4 = (bf16[80,896]{1,0:T(8,128)(2,1)}, bf16[80,896]{1,0:T(8,128)(2,1)S(1)}, u32[]{:S(2)}) copy-start(bf16[80,896]{1,0:T(8,128)(2,1)S(1)} %collective-permute-done.13.rest_2_) | copy-start | bytes 430084
  72.0 0.7 copy-start.6
  72.0 8.3 %collective-permute-start.15 = (bf16[80,896]{1,0:T(8,128)(2,1)S(1)}, bf16[80,896]{1,0:T(8,128)(2,1)S(1)}, u32[]{:S(2)}, u32[]{:S(2)}) collective-permute-start(bf16[80,896]{1,0:T(8,128)(2,1)S(1)} %collective-permute-done.12.rest_1_), channel_id=1, source_target_pairs={{0,4},{4,0},{8,12},{12,8},{16,20},{20,16},{24,28},{28,24},{1,5},{5... | collective-permute-start | bytes 430088 | tf_op jit(solution)/shard_map/ppermute | solution.py:161
  72.0 8.3 %collective-permute-start.16 = (bf16[80,896]{1,0:T(8,128)(2,1)S(1)}, bf16[80,896]{1,0:T(8,128)(2,1)S(1)}, u32[]{:S(2)}, u32[]{:S(2)}) collective-permute-start(bf16[80,896]{1,0:T(8,128)(2,1)S(1)} %collective-permute-done.13.rest_2_), channel_id=1, source_target_pairs={{0,4},{4,0},{8,12},{12,8},{16,20},{20,16},{24,28},{28,24},{1,5},{5... | collective-permute-start | bytes 430088 | tf_op jit(solution)/shard_map/ppermute | solution.py:161
  72.6 0.7 copy-start.9
  80.1 0.7 copy-start.5
  80.1 8.3 %collective-permute-start.14 = (bf16[80,896]{1,0:T(8,128)(2,1)S(1)}, bf16[80,896]{1,0:T(8,128)(2,1)S(1)}, u32[]{:S(2)}, u32[]{:S(2)}) collective-permute-start(bf16[80,896]{1,0:T(8,128)(2,1)S(1)} %collective-permute-done.10.rest_2_), channel_id=1, source_target_pairs={{0,4},{4,0},{8,12},{12,8},{16,20},{20,16},{24,28},{28,24},{1,5},{5... | collective-permute-start | bytes 430088 | tf_op jit(solution)/shard_map/ppermute | solution.py:161
  80.2 0.7 copy-start.7
  80.9 0.7 copy-start.8
  88.4 0.7 copy-start.10
  94.4 5.7 %collective-permute-start.17 = (bf16[20,2048]{1,0:T(8,128)(2,1)S(1)}, bf16[20,2048]{1,0:T(8,128)(2,1)S(1)}, u32[]{:S(2)}, u32[]{:S(2)}) collective-permute-start(bf16[20,2048]{1,0:T(8,128)(2,1)S(1)} %get-tuple-element.53), channel_id=1, source_target_pairs={{0,1},{1,0},{2,3},{3,2},{4,5},{5,4},{6,7},{7,6},{8,9},{9,8},{10,11... | collective-permute-start | bytes 245768 | tf_op jit(solution)/shard_map/ppermute | solution.py:164
  95.4 6.8 %collective-permute-start.19 = (bf16[20,2048]{1,0:T(8,128)(2,1)S(1)}, bf16[20,2048]{1,0:T(8,128)(2,1)S(1)}, u32[]{:S(2)}, u32[]{:S(2)}) collective-permute-start(bf16[20,2048]{1,0:T(8,128)(2,1)S(1)} %get-tuple-element.54), channel_id=1, source_target_pairs={{0,3},{1,2},{2,1},{3,0},{4,7},{5,6},{6,5},{7,4},{8,11},{9,10},{10,... | collective-permute-start | bytes 245768 | tf_op jit(solution)/shard_map/ppermute | solution.py:164
  96.9 6.7 %collective-permute-start.18 = (bf16[20,2048]{1,0:T(8,128)(2,1)S(1)}, bf16[20,2048]{1,0:T(8,128)(2,1)S(1)}, u32[]{:S(2)}, u32[]{:S(2)}) collective-permute-start(bf16[20,2048]{1,0:T(8,128)(2,1)S(1)} %get-tuple-element.55), channel_id=1, source_target_pairs={{0,2},{1,3},{2,0},{3,1},{4,6},{5,7},{6,4},{7,5},{8,10},{9,11},{10,... | collective-permute-start | bytes 245768 | tf_op jit(solution)/shard_map/ppermute | solution.py:164
